TPU v7x, 256 devices: a whole 4x4x8 slice. The times are simulated.
256 devices in a mesh: row: 16 (over z, core), col: 16 (over y, x).
Axes of the slice: x: 4, y: 4, z: 8, core: 2. Of those that a mesh axis runs over, the one named last changes fastest.
Arguments:
- blocks: bfloat16 [256, 32, 256, 256], P('row', 'col'), may hold values from -0.0625 to 0.0625
- block_cols: int32 [256, 32], P('row', 'col'), may hold values from 0 to 48, as said below
- objective: float32 [196608], P(('col', 'row')), may hold values from -6 to 6
- lower_bound: float32 [196608], P(('col', 'row')), may hold values from -1 to -0.2
- upper_bound: float32 [196608], P(('col', 'row')), may hold values from 0.2 to 1
- right_side: float32 [65536], P(('row', 'col')), may hold values from -6 to 6
- primal_init: float32 [196608], P(('col', 'row')), may hold values from -0.2 to 0.2
- dual_init: float32 [65536], P(('row', 'col')), may hold values from 0 to 1
Outputs:
- primal_final: float32 [196608], P(('col', 'row'))
- dual_final: float32 [65536], P(('row', 'col'))
- step_norms: float32 [8, 2], replicated
Inputs may be any that keep to these rules, and one draw needn't show every extreme that they name: `block_cols`: entry j of a row block indexes column group j // 2; its live entries (below 48) are distinct within one row block and group, 48 marks an empty slot, and in every draw some row block has all 2 slots of some group live.
All inputs are finite; a program needn't handle non-finite values.
Results may differ from a plain program's by a relative error of at most 0.0015.
Values may be sent and summed in bfloat16 or wider, within the bound.
A program may use at most 64 MiB of HBM per device.

v0:
```python
import functools
import jax
import jax.numpy as jnp
from jax import lax
from jax.sharding import Mesh
from jax.sharding import PartitionSpec as P

ITERS = 8
ROW = ("row_0", "row_1")
COL = ("col_0", "col_1")
ROW_COL = ("row_0", "row_1", "col_0", "col_1")
COL_ROW = ("col_0", "col_1", "row_0", "row_1")
step_primal = 0.5
step_dual = 0.5


def gather_turned(arrays, axis, dims):
    turned = [jnp.moveaxis(a, dim, 0) for a, dim in zip(arrays, dims)]
    both = jnp.concatenate([t.reshape(len(t), -1) for t in turned], axis=1)
    whole, at, finished = (lax.all_gather(both, axis, axis=0, tiled=True), 0, [])
    for t, dim in zip(turned, dims):
        slab = whole[:, at : at + t[0].size].reshape(-1, *t.shape[1:])
        finished.append(jnp.moveaxis(slab, 0, dim))
        at += t[0].size
    return tuple(finished)


def over_pieces(array, axis):
    tiles = lax.all_gather(array, axis)
    return tiles.sum(axis=0)


def from_everyone(array, axis):
    count = lax.axis_size(axis)
    return lax.all_to_all(
        jnp.broadcast_to(array[None], (count, *array.shape)), axis, 0, 0, tiled=True
    )


def over_copies(array, axis):
    everything = from_everyone(array, axis)
    return jnp.sum(everything, axis=0)


def over_axes(array, axes):
    return functools.reduce(lax.psum, axes, array)


def per_device(
    blocks, block_cols, objective, lower_bound, upper_bound, right_side, primal_init, dual_init
):
    row_blocks = blocks.shape[0]
    slots = blocks.shape[1]
    width = blocks.shape[2]
    row_devices = lax.axis_size(ROW)
    col_devices = lax.axis_size(COL)
    primal_len = objective.shape[0]
    dual_len = right_side.shape[0]
    col_blocks = primal_len * row_devices // width
    primal_total = float(primal_len * row_devices * col_devices)
    dual_total = float(dual_len * row_devices * col_devices)
    flat_cols = block_cols.reshape(-1)
    chosen = flat_cols[:, None] == jnp.arange(col_blocks, dtype=jnp.int32)[None, :]
    chosen_half = chosen.astype(jnp.bfloat16)
    chosen_full = chosen.astype(jnp.float32)
    history = []
    primal_slab, objective_slab, lower_slab, upper_slab = gather_turned(
        (primal_init, objective, lower_bound, upper_bound), ROW, (0, 0, 0, 0)
    )
    dual_slab, right_slab = gather_turned((dual_init, right_side), COL, (0, 0))
    primal_offset = lax.axis_index(ROW) * primal_len
    dual_offset = lax.axis_index(COL) * dual_len
    for iteration in range(ITERS):
        dual_half = dual_slab.astype(jnp.bfloat16)
        dual_amount = dual_half.shape[0] // width
        products = jnp.einsum(
            "rsab,ra->rsb",
            blocks,
            dual_half.reshape(dual_amount, width),
            preferred_element_type=jnp.float32,
        ).reshape(dual_amount * slots, width)
        gradient = over_pieces(
            jnp.dot(
                chosen_full.T,
                products,
                precision=lax.Precision.HIGHEST,
                preferred_element_type=jnp.float32,
            ).reshape(-1),
            ROW,
        )
        primal_next = jnp.minimum(
            upper_slab,
            jnp.maximum(lower_slab, primal_slab - step_primal * (objective_slab - gradient)),
        )
        extrapolated = (2.0 * primal_next - primal_slab).astype(jnp.bfloat16)
        pick_amount = extrapolated.shape[0] // width
        picked = jnp.dot(
            chosen_half,
            extrapolated.reshape(pick_amount, width),
            preferred_element_type=jnp.float32,
        )
        shaped = picked.astype(jnp.bfloat16).reshape(row_blocks, slots, width)
        image_dual = over_copies(
            jnp.einsum("rsab,rsb->ra", blocks, shaped, preferred_element_type=jnp.float32).reshape(
                -1
            ),
            COL,
        )
        dual_next = jnp.maximum(dual_slab + step_dual * (right_slab - image_dual), 0.0)
        primal_step = lax.dynamic_slice_in_dim(
            primal_next - primal_slab, primal_offset, primal_len, 0
        )
        dual_step = lax.dynamic_slice_in_dim(dual_next - dual_slab, dual_offset, dual_len, 0)
        history.append(
            jnp.stack((jnp.sum(primal_step * primal_step), jnp.sum(dual_step * dual_step)))
        )
        primal_slab = primal_next
        dual_slab = dual_next
    primal_out = lax.dynamic_slice_in_dim(primal_slab, primal_offset, primal_len, 0)
    dual_out = lax.dynamic_slice_in_dim(dual_slab, dual_offset, dual_len, 0)
    stacked = jnp.stack(history)
    stacked = over_axes(stacked, ROW_COL)
    totals = jnp.array([primal_total, dual_total], jnp.float32)
    step_norms = jnp.sqrt(stacked / totals[None, :])
    return (primal_out, dual_out, step_norms)


def solution(mesh):
    split = Mesh(mesh.devices.reshape(8, 2, 4, 4), ("row_0", "row_1", "col_0", "col_1"))
    placed = (
        P(ROW, COL, None, None),
        P(ROW, COL),
        P(COL_ROW),
        P(COL_ROW),
        P(COL_ROW),
        P(ROW_COL),
        P(COL_ROW),
        P(ROW_COL),
    )
    return jax.shard_map(
        per_device,
        mesh=split,
        in_specs=placed,
        out_specs=(P(COL_ROW), P(ROW_COL), P()),
        check_vma=False,
    )
```

profile of v0, /device:TPU:32, one launch (start us, length us, event | category | flops | bytes accessed | tf_op | source)
XLA Modules:
  0.0 402.9 jit_solution(3310335284656649400)
XLA Ops:
  2.2 23.7 %all_gather.31 = f32[4096,2]{0,1:T(2,128)S(1)} all-gather(f32[256,2]{0,1:T(2,128)S(1)} %pad_maximum_fusion.1), channel_id=1, replica_groups=mesh['row_0'=8,'row_1'=2,'col_0'=4,'col_1'=4] {'col_0','col_1'}, dimensions={0}, use_global_device_ids=true | all-gather | bytes 34816 | tf_op jit(solution)/shard_map/all_gather | solution.py:20
  29.3 20.0 %all-gather = f32[16,1,12288]{2,1,0:T(1,128)S(1)} all-gather(f32[1,1,12288]{2,1,0:T(1,128)S(1)} %reshape.329), channel_id=1, replica_groups=mesh['row_0'=8,'row_1'=2,'col_0'=4,'col_1'=4] {'row_0','row_1'}, dimensions={0}, use_global_device_ids=true | all-gather | bytes 835584 | tf_op jit(solution)/shard_map/all_gather | solution.py:29
  50.0 16.9 %all_gather.30 = f32[12288,4]{0,1:T(4,128)S(1)} all-gather(f32[768,4]{0,1:T(4,128)S(1)} %pad_maximum_fusion), channel_id=1, replica_groups=mesh['row_0'=8,'row_1'=2,'col_0'=4,'col_1'=4] {'row_0','row_1'}, dimensions={0}, use_global_device_ids=true | all-gather | bytes 208896 | tf_op jit(solution)/shard_map/all_gather | solution.py:20
  67.8 3.4 fusion.63
  72.1 4.9 %all-to-all-start = ((f32[16,1,4096]{2,1,0:T(1,128)}), f32[16,1,4096]{2,1,0:T(1,128)S(1)}, u32[]{:S(2)}, u32[]{:S(2)}) async-start(f32[16,1,4096]{2,1,0:T(1,128)} %broadcast_in_dim.59), calls=%async_computation | async-start | bytes 524288 | tf_op jit(solution)/shard_map/all_to_all | solution.py:35
  77.0 9.2 %all-to-all-done = f32[16,1,4096]{2,1,0:T(1,128)S(1)} async-done(((f32[16,1,4096]{2,1,0:T(1,128)}), f32[16,1,4096]{2,1,0:T(1,128)S(1)}, u32[]{:S(2)}, u32[]{:S(2)}) %all-to-all-start) | async-done | bytes 262176 | tf_op jit(solution)/shard_map/all_to_all | solution.py:35
  89.6 16.6 %all-gather.1 = f32[16,1,12288]{2,1,0:T(1,128)S(1)} all-gather(f32[1,1,12288]{2,1,0:T(1,128)S(1)} %reshape.331), channel_id=1, replica_groups=mesh['row_0'=8,'row_1'=2,'col_0'=4,'col_1'=4] {'row_0','row_1'}, dimensions={0}, use_global_device_ids=true | all-gather | bytes 835584 | tf_op jit(solution)/shard_map/all_gather | solution.py:29
  107.0 3.4 fusion.64
  110.6 12.1 %all_to_all.48 = f32[16,1,4096]{2,1,0:T(1,128)S(1)} all-to-all(f32[16,1,4096]{2,1,0:T(1,128)S(1)} %broadcast_in_dim.61), channel_id=1, replica_groups=mesh['row_0'=8,'row_1'=2,'col_0'=4,'col_1'=4] {'col_0','col_1'}, dimensions={0} | all-to-all | bytes 524288 | tf_op jit(solution)/shard_map/all_to_all | solution.py:35
  126.2 18.0 %all-gather.2 = f32[16,1,12288]{2,1,0:T(1,128)S(1)} all-gather(f32[1,1,12288]{2,1,0:T(1,128)S(1)} %reshape.333), channel_id=1, replica_groups=mesh['row_0'=8,'row_1'=2,'col_0'=4,'col_1'=4] {'row_0','row_1'}, dimensions={0}, use_global_device_ids=true | all-gather | bytes 835584 | tf_op jit(solution)/shard_map/all_gather | solution.py:29
  144.9 3.4 fusion.65
  148.5 12.1 %all_to_all.49 = f32[16,1,4096]{2,1,0:T(1,128)S(1)} all-to-all(f32[16,1,4096]{2,1,0:T(1,128)S(1)} %broadcast_in_dim.63), channel_id=1, replica_groups=mesh['row_0'=8,'row_1'=2,'col_0'=4,'col_1'=4] {'col_0','col_1'}, dimensions={0} | all-to-all | bytes 524288 | tf_op jit(solution)/shard_map/all_to_all | solution.py:35
  164.0 16.6 %all-gather.3 = f32[16,1,12288]{2,1,0:T(1,128)S(1)} all-gather(f32[1,1,12288]{2,1,0:T(1,128)S(1)} %reshape.335), channel_id=1, replica_groups=mesh['row_0'=8,'row_1'=2,'col_0'=4,'col_1'=4] {'row_0','row_1'}, dimensions={0}, use_global_device_ids=true | all-gather | bytes 835584 | tf_op jit(solution)/shard_map/all_gather | solution.py:29
  181.4 3.4 fusion.66
  185.7 3.7 all-to-all-start.3
  189.5 9.2 %all-to-all-done.3 = f32[16,1,4096]{2,1,0:T(1,128)S(1)} async-done(((f32[16,1,4096]{2,1,0:T(1,128)}), f32[16,1,4096]{2,1,0:T(1,128)S(1)}, u32[]{:S(2)}, u32[]{:S(2)}) %all-to-all-start.3) | async-done | bytes 262176 | tf_op jit(solution)/shard_map/all_to_all | solution.py:35
  202.2 18.0 %all-gather.4 = f32[16,1,12288]{2,1,0:T(1,128)S(1)} all-gather(f32[1,1,12288]{2,1,0:T(1,128)S(1)} %reshape.337), channel_id=1, replica_groups=mesh['row_0'=8,'row_1'=2,'col_0'=4,'col_1'=4] {'row_0','row_1'}, dimensions={0}, use_global_device_ids=true | all-gather | bytes 835584 | tf_op jit(solution)/shard_map/all_gather | solution.py:29
  225.2 3.5 all-to-all-start.4
  228.7 9.4 %all-to-all-done.4 = f32[16,1,4096]{2,1,0:T(1,128)S(1)} async-done(((f32[16,1,4096]{2,1,0:T(1,128)}), f32[16,1,4096]{2,1,0:T(1,128)S(1)}, u32[]{:S(2)}, u32[]{:S(2)}) %all-to-all-start.4) | async-done | bytes 262176 | tf_op jit(solution)/shard_map/all_to_all | solution.py:35
  241.6 16.6 %all-gather.5 = f32[16,1,12288]{2,1,0:T(1,128)S(1)} all-gather(f32[1,1,12288]{2,1,0:T(1,128)S(1)} %reshape.339), channel_id=1, replica_groups=mesh['row_0'=8,'row_1'=2,'col_0'=4,'col_1'=4] {'row_0','row_1'}, dimensions={0}, use_global_device_ids=true | all-gather | bytes 835584 | tf_op jit(solution)/shard_map/all_gather | solution.py:29
  263.3 3.5 all-to-all-start.5
  266.9 9.4 %all-to-all-done.5 = f32[16,1,4096]{2,1,0:T(1,128)S(1)} async-done(((f32[16,1,4096]{2,1,0:T(1,128)}), f32[16,1,4096]{2,1,0:T(1,128)S(1)}, u32[]{:S(2)}, u32[]{:S(2)}) %all-to-all-start.5) | async-done | bytes 262176 | tf_op jit(solution)/shard_map/all_to_all | solution.py:35
  279.7 18.0 %all-gather.6 = f32[16,1,12288]{2,1,0:T(1,128)S(1)} all-gather(f32[1,1,12288]{2,1,0:T(1,128)S(1)} %reshape.341), channel_id=1, replica_groups=mesh['row_0'=8,'row_1'=2,'col_0'=4,'col_1'=4] {'row_0','row_1'}, dimensions={0}, use_global_device_ids=true | all-gather | bytes 835584 | tf_op jit(solution)/shard_map/all_gather | solution.py:29
  302.7 3.5 all-to-all-start.6
  306.3 9.4 %all-to-all-done.6 = f32[16,1,4096]{2,1,0:T(1,128)S(1)} async-done(((f32[16,1,4096]{2,1,0:T(1,128)}), f32[16,1,4096]{2,1,0:T(1,128)S(1)}, u32[]{:S(2)}, u32[]{:S(2)}) %all-to-all-start.6) | async-done | bytes 262176 | tf_op jit(solution)/shard_map/all_to_all | solution.py:35
  319.2 16.6 %all-gather.7 = f32[16,1,12288]{2,1,0:T(1,128)S(1)} all-gather(f32[1,1,12288]{2,1,0:T(1,128)S(1)} %reshape.343), channel_id=1, replica_groups=mesh['row_0'=8,'row_1'=2,'col_0'=4,'col_1'=4] {'row_0','row_1'}, dimensions={0}, use_global_device_ids=true | all-gather | bytes 835584 | tf_op jit(solution)/shard_map/all_gather | solution.py:29
  336.6 3.4 fusion.70
  340.9 3.5 all-to-all-start.7
  345.8 8.0 %all-to-all-done.7 = f32[16,1,4096]{2,1,0:T(1,128)S(1)} async-done(((f32[16,1,4096]{2,1,0:T(1,128)}), f32[16,1,4096]{2,1,0:T(1,128)S(1)}, u32[]{:S(2)}, u32[]{:S(2)}) %all-to-all-start.7) | async-done | bytes 262176 | tf_op jit(solution)/shard_map/all_to_all | solution.py:35
  366.8 15.8 %psum.28 = f32[8,2]{0,1:T(2,128)S(1)} all-reduce(f32[8,2]{0,1:T(2,128)S(1)} %stack.131), channel_id=1, replica_groups=mesh['row_0'=8,'row_1'=2,'col_0'=4,'col_1'=4] {'row_0'}, use_global_device_ids=true, to_apply=%region_32.0 | all-reduce | flops 16 | bytes 128 | tf_op jit(solution)/shard_map/psum | solution.py:46
  385.1 8.5 %psum.30 = f32[8,2]{0,1:T(2,128)S(1)} all-reduce(f32[8,2]{0,1:T(2,128)S(1)} %psum.29), channel_id=1, replica_groups=mesh['row_0'=8,'row_1'=2,'col_0'=4,'col_1'=4] {'col_0'}, use_global_device_ids=true, to_apply=%region_34.0 | all-reduce | flops 16 | bytes 128 | tf_op jit(solution)/shard_map/psum | solution.py:46
  393.6 8.6 %psum.31 = f32[8,2]{0,1:T(2,128)S(1)} all-reduce(f32[8,2]{0,1:T(2,128)S(1)} %psum.30), channel_id=1, replica_groups=mesh['row_0'=8,'row_1'=2,'col_0'=4,'col_1'=4] {'col_1'}, use_global_device_ids=true, to_apply=%region_35.0 | all-reduce | flops 16 | bytes 128 | tf_op jit(solution)/shard_map/psum | solution.py:46
  (175 shorter events, 69.1 us)
Async XLA Ops:
  0.6 49.2 %copy-start = (f32[768]{0:T(1024)S(1)}, f32[768]{0:T(1024)}, u32[]{:S(2)}) copy-start(f32[768]{0:T(1024)} %param.15) | copy-start | bytes 9220
  0.6 49.2 %copy-start.1 = (f32[768]{0:T(1024)S(1)}, f32[768]{0:T(1024)}, u32[]{:S(2)}) copy-start(f32[768]{0:T(1024)} %param.11) | copy-start | bytes 9220
  0.7 49.2 %copy-start.2 = (f32[768]{0:T(1024)S(1)}, f32[768]{0:T(1024)}, u32[]{:S(2)}) copy-start(f32[768]{0:T(1024)} %param.12) | copy-start | bytes 9220
  0.7 49.3 %copy-start.3 = (f32[768]{0:T(1024)S(1)}, f32[768]{0:T(1024)}, u32[]{:S(2)}) copy-start(f32[768]{0:T(1024)} %param.13) | copy-start | bytes 9220
  72.1 14.1 %all-to-all-start = ((f32[16,1,4096]{2,1,0:T(1,128)}), f32[16,1,4096]{2,1,0:T(1,128)S(1)}, u32[]{:S(2)}, u32[]{:S(2)}) async-start(f32[16,1,4096]{2,1,0:T(1,128)} %broadcast_in_dim.59), calls=%async_computation | async-start | bytes 524288 | tf_op jit(solution)/shard_map/all_to_all | solution.py:35
  185.7 13.0 %all-to-all-start.3 = ((f32[16,1,4096]{2,1,0:T(1,128)}), f32[16,1,4096]{2,1,0:T(1,128)S(1)}, u32[]{:S(2)}, u32[]{:S(2)}) async-start(f32[16,1,4096]{2,1,0:T(1,128)} %broadcast_in_dim.65), calls=%async_computation.3 | async-start | bytes 524288 | tf_op jit(solution)/shard_map/all_to_all | solution.py:35
  225.2 13.0 %all-to-all-start.4 = ((f32[16,1,4096]{2,1,0:T(1,128)}), f32[16,1,4096]{2,1,0:T(1,128)S(1)}, u32[]{:S(2)}, u32[]{:S(2)}) async-start(f32[16,1,4096]{2,1,0:T(1,128)} %broadcast_in_dim.67), calls=%async_computation.4 | async-start | bytes 524288 | tf_op jit(solution)/shard_map/all_to_all | solution.py:35
  263.3 13.0 %all-to-all-start.5 = ((f32[16,1,4096]{2,1,0:T(1,128)}), f32[16,1,4096]{2,1,0:T(1,128)S(1)}, u32[]{:S(2)}, u32[]{:S(2)}) async-start(f32[16,1,4096]{2,1,0:T(1,128)} %broadcast_in_dim.69), calls=%async_computation.5 | async-start | bytes 524288 | tf_op jit(solution)/shard_map/all_to_all | solution.py:35
  302.7 13.0 %all-to-all-start.6 = ((f32[16,1,4096]{2,1,0:T(1,128)}), f32[16,1,4096]{2,1,0:T(1,128)S(1)}, u32[]{:S(2)}, u32[]{:S(2)}) async-start(f32[16,1,4096]{2,1,0:T(1,128)} %broadcast_in_dim.71), calls=%async_computation.6 | async-start | bytes 524288 | tf_op jit(solution)/shard_map/all_to_all | solution.py:35
  319.2 83.1 %copy-start.4 = (f32[2]{0:T(128)S(1)}, f32[2]{0:T(128)}, u32[]{:S(2)}) copy-start(f32[2]{0:T(128)} %constant.46) | copy-start | bytes 28
  340.9 13.0 %all-to-all-start.7 = ((f32[16,1,4096]{2,1,0:T(1,128)}), f32[16,1,4096]{2,1,0:T(1,128)S(1)}, u32[]{:S(2)}, u32[]{:S(2)}) async-start(f32[16,1,4096]{2,1,0:T(1,128)} %broadcast_in_dim.73), calls=%async_computation.7 | async-start | bytes 524288 | tf_op jit(solution)/shard_map/all_to_all | solution.py:35
where the time goes:
time: 405 us; the launch traced here: 403 us
  blocking collectives  241 us (60%)
  waiting for transfers between devices  54.6 us (13%)
  matrix products  53.5 us (13%)
  starting transfers between devices  22.8 us (6%)
  other arithmetic  20.5 us (5%)
  local copies, waits for them, and re-layouts  9.56 us (2%)
    all_gather x8, blocking collectives, over_pieces(): tiles = lax.all_gather(array, axis)  140 us
    all_to_all x6, waiting for transfers between devices, from_everyone(): lax.all_to_all(jnp.broadcast_to(array[None], (count, *array.shape)), axis...  54.6 us
    all_gather x2, blocking collectives, gather_turned(): lax.all_gather(both, axis, axis=0, tiled=True)  40.6 us
    psum x4, blocking collectives, over_axes(): return functools.reduce(lax.psum, axes, array)  35.4 us
    dot_general x8, matrix products, per_device(): jnp.einsum('rsab,rsb->ra', blocks, shaped, preferred_element_type=jnp.flo...  26.9 us
    all_to_all x2, blocking collectives, from_everyone(): lax.all_to_all(jnp.broadcast_to(array[None], (count, *array.shape)), axis...  24.2 us
    all_to_all x6, starting transfers between devices, from_everyone(): lax.all_to_all(jnp.broadcast_to(array[None], (count, *array.shape)), axis...  22.8 us
    dot_general x8, matrix products, per_device(): jnp.einsum('rsab,ra->rsb', blocks, dual_half.reshape(dual_amount, width),...  22.7 us
  transfers between devices with their start and end apart: 6, of which 6 were waited for; matrix products, arithmetic and copies ran while one was open for 0% of the time, Pallas kernels for 0%

commit v1 on v0

--- a/solution.py
+++ b/solution.py
@@ -17,7 +17,13 @@
 def gather_turned(arrays, axis, dims):
     turned = [jnp.moveaxis(a, dim, 0) for a, dim in zip(arrays, dims)]
     both = jnp.concatenate([t.reshape(len(t), -1) for t in turned], axis=1)
-    whole, at, finished = (lax.all_gather(both, axis, axis=0, tiled=True), 0, [])
+    whole, at, finished = (
+        jnp.concatenate(
+            lax.all_to_all(jnp.stack([both] * lax.axis_size(axis)), axis, 0, 0), axis=0
+        ),
+        0,
+        [],
+    )
     for t, dim in zip(turned, dims):
         slab = whole[:, at : at + t[0].size].reshape(-1, *t.shape[1:])
         finished.append(jnp.moveaxis(slab, 0, dim))

time: 405 us -> 386 us (0.953)
  blocking collectives: 241 us -> 199 us
  starting transfers between devices: 22.8 us -> 37 us
  waiting for transfers between devices: 54.6 us -> 58.9 us
    all_gather x2 -> x0, blocking collectives: 40.6 us -> none  [gather_turned(): lax.all_gather(both, axis, axis=0, tiled=True)]
    all_to_all x0 -> x2, starting transfers between devices: none -> 15.6 us  [gather_turned(): lax.all_to_all(jnp.stack([both] * lax.axis_size(axis)), axis, 0, 0)]
  transfers between devices with their start and end apart: 6 -> 8, of which waited for: 6 -> 7; matrix products, arithmetic and copies ran while one was open for 0% -> 2% of each run, Pallas kernels for 0% -> 0%
where the time goes in v1:
time: 386 us; the launch traced here: 383 us
  blocking collectives  199 us (52%)
  waiting for transfers between devices  58.9 us (15%)
  matrix products  53.5 us (14%)
  starting transfers between devices  37 us (10%)
  other arithmetic  20.5 us (5%)
  local copies, waits for them, and re-layouts  13.6 us (4%)
    all_gather x8, blocking collectives, over_pieces(): tiles = lax.all_gather(array, axis)  140 us
    all_to_all x6, waiting for transfers between devices, from_everyone(): lax.all_to_all(jnp.broadcast_to(array[None], (count, *array.shape)), axis...  54.9 us
    psum x4, blocking collectives, over_axes(): return functools.reduce(lax.psum, axes, array)  34.9 us
    dot_general x8, matrix products, per_device(): jnp.einsum('rsab,rsb->ra', blocks, shaped, preferred_element_type=jnp.flo...  26.9 us
    all_to_all x2, blocking collectives, from_everyone(): lax.all_to_all(jnp.broadcast_to(array[None], (count, *array.shape)), axis...  24.2 us
    dot_general x8, matrix products, per_device(): jnp.einsum('rsab,ra->rsb', blocks, dual_half.reshape(dual_amount, width),...  22.7 us
    all_to_all x6, starting transfers between devices, from_everyone(): lax.all_to_all(jnp.broadcast_to(array[None], (count, *array.shape)), axis...  21.4 us
    all_to_all x2, starting transfers between devices, gather_turned(): lax.all_to_all(jnp.stack([both] * lax.axis_size(axis)), axis, 0, 0)  15.6 us
  transfers between devices with their start and end apart: 8, of which 7 were waited for; matrix products, arithmetic and copies ran while one was open for 2% of the time, Pallas kernels for 0%

profile of v1, /device:TPU:32, one launch (start us, length us, event | category | flops | bytes accessed | tf_op | source)
XLA Modules:
  0.0 383.3 jit_solution(743928312672725123)
XLA Ops:
  1.9 7.0 %all-to-all-start.1 = ((f32[16,256,2]{1,2,0:T(2,128)}), f32[16,256,2]{1,2,0:T(2,128)S(1)}, u32[]{:S(2)}, u32[]{:S(2)}) async-start(f32[16,256,2]{1,2,0:T(2,128)} %stack.138), calls=%async_computation.1 | async-start | bytes 65536 | tf_op jit(solution)/shard_map/all_to_all | solution.py:22
  12.6 4.0 %all-to-all-done.1 = f32[16,256,2]{1,2,0:T(2,128)S(1)} async-done(((f32[16,256,2]{1,2,0:T(2,128)}), f32[16,256,2]{1,2,0:T(2,128)S(1)}, u32[]{:S(2)}, u32[]{:S(2)}) %all-to-all-start.1) | async-done | bytes 32800 | tf_op jit(solution)/shard_map/all_to_all | solution.py:22
  17.3 8.6 %all-to-all-start = ((f32[16,768,4]{1,2,0:T(4,128)}), f32[16,768,4]{1,2,0:T(4,128)S(1)}, u32[]{:S(2)}, u32[]{:S(2)}) async-start(f32[16,768,4]{1,2,0:T(4,128)} %stack.137), calls=%async_computation | async-start | bytes 393216 | tf_op jit(solution)/shard_map/all_to_all | solution.py:22
  29.2 17.9 %all-gather = f32[16,1,12288]{2,1,0:T(1,128)S(1)} all-gather(f32[1,1,12288]{2,1,0:T(1,128)S(1)} %reshape.341), channel_id=1, replica_groups=mesh['row_0'=8,'row_1'=2,'col_0'=4,'col_1'=4] {'row_0','row_1'}, dimensions={0}, use_global_device_ids=true | all-gather | bytes 835584 | tf_op jit(solution)/shard_map/all_gather | solution.py:35
  48.6 3.4 fusion.63
  52.9 3.5 all-to-all-start.2
  56.4 9.4 %all-to-all-done.2 = f32[16,1,4096]{2,1,0:T(1,128)S(1)} async-done(((f32[16,1,4096]{2,1,0:T(1,128)}), f32[16,1,4096]{2,1,0:T(1,128)S(1)}, u32[]{:S(2)}, u32[]{:S(2)}) %all-to-all-start.2) | async-done | bytes 262176 | tf_op jit(solution)/shard_map/all_to_all | solution.py:41
  69.3 17.9 %all-gather.1 = f32[16,1,12288]{2,1,0:T(1,128)S(1)} all-gather(f32[1,1,12288]{2,1,0:T(1,128)S(1)} %reshape.343), channel_id=1, replica_groups=mesh['row_0'=8,'row_1'=2,'col_0'=4,'col_1'=4] {'row_0','row_1'}, dimensions={0}, use_global_device_ids=true | all-gather | bytes 835584 | tf_op jit(solution)/shard_map/all_gather | solution.py:35
  88.0 3.4 fusion.64
  91.6 12.1 %all_to_all.58 = f32[16,1,4096]{2,1,0:T(1,128)S(1)} all-to-all(f32[16,1,4096]{2,1,0:T(1,128)S(1)} %broadcast_in_dim.61), channel_id=1, replica_groups=mesh['row_0'=8,'row_1'=2,'col_0'=4,'col_1'=4] {'col_0','col_1'}, dimensions={0} | all-to-all | bytes 524288 | tf_op jit(solution)/shard_map/all_to_all | solution.py:41
  107.2 17.4 %all-gather.2 = f32[16,1,12288]{2,1,0:T(1,128)S(1)} all-gather(f32[1,1,12288]{2,1,0:T(1,128)S(1)} %reshape.345), channel_id=1, replica_groups=mesh['row_0'=8,'row_1'=2,'col_0'=4,'col_1'=4] {'row_0','row_1'}, dimensions={0}, use_global_device_ids=true | all-gather | bytes 835584 | tf_op jit(solution)/shard_map/all_gather | solution.py:35
  125.3 3.4 fusion.65
  128.9 12.1 %all_to_all.59 = f32[16,1,4096]{2,1,0:T(1,128)S(1)} all-to-all(f32[16,1,4096]{2,1,0:T(1,128)S(1)} %broadcast_in_dim.63), channel_id=1, replica_groups=mesh['row_0'=8,'row_1'=2,'col_0'=4,'col_1'=4] {'col_0','col_1'}, dimensions={0} | all-to-all | bytes 524288 | tf_op jit(solution)/shard_map/all_to_all | solution.py:41
  144.5 17.2 %all-gather.3 = f32[16,1,12288]{2,1,0:T(1,128)S(1)} all-gather(f32[1,1,12288]{2,1,0:T(1,128)S(1)} %reshape.347), channel_id=1, replica_groups=mesh['row_0'=8,'row_1'=2,'col_0'=4,'col_1'=4] {'row_0','row_1'}, dimensions={0}, use_global_device_ids=true | all-gather | bytes 835584 | tf_op jit(solution)/shard_map/all_gather | solution.py:35
  166.7 3.7 all-to-all-start.5
  170.4 9.2 %all-to-all-done.5 = f32[16,1,4096]{2,1,0:T(1,128)S(1)} async-done(((f32[16,1,4096]{2,1,0:T(1,128)}), f32[16,1,4096]{2,1,0:T(1,128)S(1)}, u32[]{:S(2)}, u32[]{:S(2)}) %all-to-all-start.5) | async-done | bytes 262176 | tf_op jit(solution)/shard_map/all_to_all | solution.py:41
  183.1 17.4 %all-gather.4 = f32[16,1,12288]{2,1,0:T(1,128)S(1)} all-gather(f32[1,1,12288]{2,1,0:T(1,128)S(1)} %reshape.349), channel_id=1, replica_groups=mesh['row_0'=8,'row_1'=2,'col_0'=4,'col_1'=4] {'row_0','row_1'}, dimensions={0}, use_global_device_ids=true | all-gather | bytes 835584 | tf_op jit(solution)/shard_map/all_gather | solution.py:35
  205.6 3.5 all-to-all-start.6
  209.2 9.4 %all-to-all-done.6 = f32[16,1,4096]{2,1,0:T(1,128)S(1)} async-done(((f32[16,1,4096]{2,1,0:T(1,128)}), f32[16,1,4096]{2,1,0:T(1,128)S(1)}, u32[]{:S(2)}, u32[]{:S(2)}) %all-to-all-start.6) | async-done | bytes 262176 | tf_op jit(solution)/shard_map/all_to_all | solution.py:41
  222.0 17.2 %all-gather.5 = f32[16,1,12288]{2,1,0:T(1,128)S(1)} all-gather(f32[1,1,12288]{2,1,0:T(1,128)S(1)} %reshape.351), channel_id=1, replica_groups=mesh['row_0'=8,'row_1'=2,'col_0'=4,'col_1'=4] {'row_0','row_1'}, dimensions={0}, use_global_device_ids=true | all-gather | bytes 835584 | tf_op jit(solution)/shard_map/all_gather | solution.py:35
  244.2 3.5 all-to-all-start.7
  247.8 9.4 %all-to-all-done.7 = f32[16,1,4096]{2,1,0:T(1,128)S(1)} async-done(((f32[16,1,4096]{2,1,0:T(1,128)}), f32[16,1,4096]{2,1,0:T(1,128)S(1)}, u32[]{:S(2)}, u32[]{:S(2)}) %all-to-all-start.7) | async-done | bytes 262176 | tf_op jit(solution)/shard_map/all_to_all | solution.py:41
  260.7 17.4 %all-gather.6 = f32[16,1,12288]{2,1,0:T(1,128)S(1)} all-gather(f32[1,1,12288]{2,1,0:T(1,128)S(1)} %reshape.353), channel_id=1, replica_groups=mesh['row_0'=8,'row_1'=2,'col_0'=4,'col_1'=4] {'row_0','row_1'}, dimensions={0}, use_global_device_ids=true | all-gather | bytes 835584 | tf_op jit(solution)/shard_map/all_gather | solution.py:35
  283.2 3.5 all-to-all-start.8
  286.7 9.4 %all-to-all-done.8 = f32[16,1,4096]{2,1,0:T(1,128)S(1)} async-done(((f32[16,1,4096]{2,1,0:T(1,128)}), f32[16,1,4096]{2,1,0:T(1,128)S(1)}, u32[]{:S(2)}, u32[]{:S(2)}) %all-to-all-start.8) | async-done | bytes 262176 | tf_op jit(solution)/shard_map/all_to_all | solution.py:41
  299.6 17.2 %all-gather.7 = f32[16,1,12288]{2,1,0:T(1,128)S(1)} all-gather(f32[1,1,12288]{2,1,0:T(1,128)S(1)} %reshape.355), channel_id=1, replica_groups=mesh['row_0'=8,'row_1'=2,'col_0'=4,'col_1'=4] {'row_0','row_1'}, dimensions={0}, use_global_device_ids=true | all-gather | bytes 835584 | tf_op jit(solution)/shard_map/all_gather | solution.py:35
  317.5 3.4 fusion.70
  321.8 3.5 all-to-all-start.9
  326.8 8.0 %all-to-all-done.9 = f32[16,1,4096]{2,1,0:T(1,128)S(1)} async-done(((f32[16,1,4096]{2,1,0:T(1,128)}), f32[16,1,4096]{2,1,0:T(1,128)S(1)}, u32[]{:S(2)}, u32[]{:S(2)}) %all-to-all-start.9) | async-done | bytes 262176 | tf_op jit(solution)/shard_map/all_to_all | solution.py:41
  347.8 15.3 %psum.28 = f32[8,2]{0,1:T(2,128)S(1)} all-reduce(f32[8,2]{0,1:T(2,128)S(1)} %stack.171), channel_id=1, replica_groups=mesh['row_0'=8,'row_1'=2,'col_0'=4,'col_1'=4] {'row_0'}, use_global_device_ids=true, to_apply=%region_32.0 | all-reduce | flops 16 | bytes 128 | tf_op jit(solution)/shard_map/psum | solution.py:52
  365.5 8.5 %psum.30 = f32[8,2]{0,1:T(2,128)S(1)} all-reduce(f32[8,2]{0,1:T(2,128)S(1)} %psum.29), channel_id=1, replica_groups=mesh['row_0'=8,'row_1'=2,'col_0'=4,'col_1'=4] {'col_0'}, use_global_device_ids=true, to_apply=%region_34.0 | all-reduce | flops 16 | bytes 128 | tf_op jit(solution)/shard_map/psum | solution.py:52
  374.1 8.6 %psum.31 = f32[8,2]{0,1:T(2,128)S(1)} all-reduce(f32[8,2]{0,1:T(2,128)S(1)} %psum.30), channel_id=1, replica_groups=mesh['row_0'=8,'row_1'=2,'col_0'=4,'col_1'=4] {'col_1'}, use_global_device_ids=true, to_apply=%region_35.0 | all-reduce | flops 16 | bytes 128 | tf_op jit(solution)/shard_map/psum | solution.py:52
  (171 shorter events, 76.5 us)
Async XLA Ops:
  1.9 14.6 %all-to-all-start.1 = ((f32[16,256,2]{1,2,0:T(2,128)}), f32[16,256,2]{1,2,0:T(2,128)S(1)}, u32[]{:S(2)}, u32[]{:S(2)}) async-start(f32[16,256,2]{1,2,0:T(2,128)} %stack.138), calls=%async_computation.1 | async-start | bytes 65536 | tf_op jit(solution)/shard_map/all_to_all | solution.py:22
  17.3 30.4 %all-to-all-start = ((f32[16,768,4]{1,2,0:T(4,128)}), f32[16,768,4]{1,2,0:T(4,128)S(1)}, u32[]{:S(2)}, u32[]{:S(2)}) async-start(f32[16,768,4]{1,2,0:T(4,128)} %stack.137), calls=%async_computation | async-start | bytes 393216 | tf_op jit(solution)/shard_map/all_to_all | solution.py:22
  52.9 13.0 %all-to-all-start.2 = ((f32[16,1,4096]{2,1,0:T(1,128)}), f32[16,1,4096]{2,1,0:T(1,128)S(1)}, u32[]{:S(2)}, u32[]{:S(2)}) async-start(f32[16,1,4096]{2,1,0:T(1,128)} %broadcast_in_dim.59), calls=%async_computation.2 | async-start | bytes 524288 | tf_op jit(solution)/shard_map/all_to_all | solution.py:41
  166.7 13.0 %all-to-all-start.5 = ((f32[16,1,4096]{2,1,0:T(1,128)}), f32[16,1,4096]{2,1,0:T(1,128)S(1)}, u32[]{:S(2)}, u32[]{:S(2)}) async-start(f32[16,1,4096]{2,1,0:T(1,128)} %broadcast_in_dim.65), calls=%async_computation.5 | async-start | bytes 524288 | tf_op jit(solution)/shard_map/all_to_all | solution.py:41
  205.6 13.0 %all-to-all-start.6 = ((f32[16,1,4096]{2,1,0:T(1,128)}), f32[16,1,4096]{2,1,0:T(1,128)S(1)}, u32[]{:S(2)}, u32[]{:S(2)}) async-start(f32[16,1,4096]{2,1,0:T(1,128)} %broadcast_in_dim.67), calls=%async_computation.6 | async-start | bytes 524288 | tf_op jit(solution)/shard_map/all_to_all | solution.py:41
  244.2 13.0 %all-to-all-start.7 = ((f32[16,1,4096]{2,1,0:T(1,128)}), f32[16,1,4096]{2,1,0:T(1,128)S(1)}, u32[]{:S(2)}, u32[]{:S(2)}) async-start(f32[16,1,4096]{2,1,0:T(1,128)} %broadcast_in_dim.69), calls=%async_computation.7 | async-start | bytes 524288 | tf_op jit(solution)/shard_map/all_to_all | solution.py:41
  283.2 13.0 %all-to-all-start.8 = ((f32[16,1,4096]{2,1,0:T(1,128)}), f32[16,1,4096]{2,1,0:T(1,128)S(1)}, u32[]{:S(2)}, u32[]{:S(2)}) async-start(f32[16,1,4096]{2,1,0:T(1,128)} %broadcast_in_dim.71), calls=%async_computation.8 | async-start | bytes 524288 | tf_op jit(solution)/shard_map/all_to_all | solution.py:41
  299.6 83.1 %copy-start = (f32[2]{0:T(128)S(1)}, f32[2]{0:T(128)}, u32[]{:S(2)}) copy-start(f32[2]{0:T(128)} %constant.46) | copy-start | bytes 28
  321.8 13.0 %all-to-all-start.9 = ((f32[16,1,4096]{2,1,0:T(1,128)}), f32[16,1,4096]{2,1,0:T(1,128)S(1)}, u32[]{:S(2)}, u32[]{:S(2)}) async-start(f32[16,1,4096]{2,1,0:T(1,128)} %broadcast_in_dim.73), calls=%async_computation.9 | async-start | bytes 524288 | tf_op jit(solution)/shard_map/all_to_all | solution.py:41
